TPU v7x, 32 devices: a whole 2x2x4 slice. The times are simulated.
32 devices in a mesh: chan: 4 (over y, x), slab: 8 (over z, core).
Axes of the slice: x: 2, y: 2, z: 4, core: 2. Of those that a mesh axis runs over, the one named last changes fastest.
Arguments:
- taylor_models: float32 [2, 2048, 2048], P(None, 'slab', 'chan'), may hold values from -6 to 6
- gridded_vis: bfloat16 [4, 2, 2048, 2048], P('chan', None, 'slab'), may hold values from -6 to 6
- uv_weight: bfloat16 [4, 2048, 2048], P('chan', 'slab'), may hold values from 0 to 2
- freq_ratio: float32 [4], P('chan'), may hold values from 0.6 to 1.4
- robust_scale: float32 [4], P('chan'), may hold values from 0.25 to 4
Outputs:
- taylor_residual: float32 [2, 2048, 2048], P(None, 'slab', 'chan')
All inputs are finite; a program needn't handle non-finite values.
Results may differ from a plain program's by a relative error of at most 0.0003.
Values sent between devices are 32-bit elements; how exact they have to be, the bound alone decides.
No kernel may reach another device: no remote copies, remote signals or barrier semaphores. Data moves between devices by JAX's collectives and lax.ppermute only.
A program may use at most 64 MiB of HBM per device.

v0:
```python
import math

import jax
import jax.numpy as jnp
from jax import lax
from jax.sharding import PartitionSpec as P

PIX = 2048
TERMS = 2


HIGHEST = lax.Precision.HIGHEST


def dft_table(points, direction):
    steps_all = jnp.arange(points, dtype=jnp.int32)
    product = steps_all[:, None] * steps_all[None, :] % points
    angles = product.astype(jnp.float32) * (2.0 * math.pi / points)
    return (jnp.cos(angles), direction * jnp.sin(angles))


def twiddle_table(outer_points, inner_points, direction):
    outer_steps = jnp.arange(outer_points, dtype=jnp.int32)
    inner_steps = jnp.arange(inner_points, dtype=jnp.int32)
    overall = outer_points * inner_points
    product = outer_steps[:, None] * inner_steps[None, :] % overall
    angles = product.astype(jnp.float32) * (2.0 * math.pi / overall)
    return (jnp.cos(angles), direction * jnp.sin(angles))


def complex_product(formula, left_real, left_imag, table_real, table_imag):
    out_real = jnp.einsum(formula, left_real, table_real, precision=HIGHEST) - jnp.einsum(
        formula, left_imag, table_imag, precision=HIGHEST
    )
    out_imag = jnp.einsum(formula, left_real, table_imag, precision=HIGHEST) + jnp.einsum(
        formula, left_imag, table_real, precision=HIGHEST
    )
    return (out_real, out_imag)


def rotate(left_real, left_imag, table_real, table_imag):
    return (
        left_real * table_real - left_imag * table_imag,
        left_real * table_imag + left_imag * table_real,
    )


def local(taylor_models, gridded_vis, uv_weight, freq_ratio, robust_scale):
    inner_count = 128
    outer_count = PIX // inner_count
    models = lax.all_gather(taylor_models, "chan", axis=2, tiled=True)
    row_count = models.shape[1]
    outer_cos, outer_sin = dft_table(outer_count, -1.0)
    inner_cos, inner_sin = dft_table(inner_count, -1.0)
    twist_cos, twist_sin = twiddle_table(outer_count, inner_count, -1.0)
    offset = freq_ratio[0] - 1.0
    sky_image = models[0]
    term_index = 1
    sky_image = sky_image + offset**term_index * models[term_index]
    layered = sky_image.reshape(row_count, outer_count, inner_count)
    part_real = jnp.einsum("yba,jb->yja", layered, outer_cos, precision=HIGHEST)
    part_imag = jnp.einsum("yba,jb->yja", layered, outer_sin, precision=HIGHEST)
    turned_real, turned_imag = rotate(part_real, part_imag, twist_cos, twist_sin)
    spec_real, spec_imag = complex_product(
        "yja,ka->kjy", turned_real, turned_imag, inner_cos, inner_sin
    )
    outgoing = jnp.stack([spec_real, spec_imag]).reshape(2, PIX, row_count)
    columns = lax.all_to_all(outgoing, "slab", split_axis=1, concat_axis=2, tiled=True)
    col_count = columns.shape[1]
    layered_cols = columns.reshape(2, col_count, outer_count, inner_count)
    part_real, part_imag = complex_product(
        "uba,jb->uja", layered_cols[0], layered_cols[1], outer_cos, outer_sin
    )
    turned_real, turned_imag = rotate(part_real, part_imag, twist_cos, twist_sin)
    freq_real, freq_imag = complex_product(
        "uja,ka->ujk", turned_real, turned_imag, inner_cos, inner_sin
    )
    freq_real = freq_real / PIX
    freq_imag = freq_imag / PIX
    weight = (
        uv_weight[0]
        .astype(jnp.float32)
        .reshape(col_count, inner_count, outer_count)
        .transpose(0, 2, 1)
    )
    visible = (
        gridded_vis[0]
        .astype(jnp.float32)
        .reshape(2, col_count, inner_count, outer_count)
        .transpose(0, 1, 3, 2)
    )
    delta_real = visible[0] - weight * freq_real
    delta_imag = visible[1] - weight * freq_imag
    robust = 1.0 / (1.0 + robust_scale[0] * (delta_real * delta_real + delta_imag * delta_imag))
    weighted_real = robust * delta_real
    weighted_imag = robust * delta_imag
    back_real, back_imag = complex_product(
        "ujk,ak->uja", weighted_real, weighted_imag, inner_cos, -inner_sin
    )
    back_real, back_imag = rotate(back_real, back_imag, twist_cos, -twist_sin)
    back_real, back_imag = complex_product(
        "uja,bj->uba", back_real, back_imag, outer_cos, -outer_sin
    )
    outgoing_back = jnp.stack([back_real, back_imag]).reshape(2, col_count, PIX)
    returned = lax.all_to_all(outgoing_back, "slab", split_axis=2, concat_axis=1, tiled=True)
    layered_rows = returned.reshape(2, inner_count, outer_count, row_count)
    last_real, last_imag = complex_product(
        "kjy,ak->ajy", layered_rows[0], layered_rows[1], inner_cos, -inner_sin
    )
    last_real, last_imag = rotate(
        last_real, last_imag, twist_cos.T[:, :, None], -twist_sin.T[:, :, None]
    )
    image_out = jnp.einsum("ajy,bj->yba", last_real, outer_cos, precision=HIGHEST) + jnp.einsum(
        "ajy,bj->yba", last_imag, outer_sin, precision=HIGHEST
    )
    residuals = [image_out.reshape(row_count, PIX) / PIX]
    offsets = [offset]
    stacked_res = jnp.stack(residuals)
    chan_count = lax.axis_size("chan")
    coeffs = jnp.broadcast_to(
        jnp.stack(offsets)[:, None, None], (stacked_res.shape[0], 1, chan_count)
    )
    tiles, offsets_all = (
        lax.all_to_all(stacked_res, "chan", split_axis=2, concat_axis=0, tiled=True),
        lax.all_to_all(coeffs, "chan", split_axis=2, concat_axis=0, tiled=True),
    )
    layers = []
    for term_index in range(TERMS):
        layers.append(jnp.sum(tiles * offsets_all**term_index, axis=0))
    return jnp.stack(layers)


def solution(mesh):
    placed = (
        P(None, "slab", "chan"),
        P("chan", None, "slab", None),
        P("chan", "slab", None),
        P("chan"),
        P("chan"),
    )
    return jax.shard_map(
        local, mesh=mesh, in_specs=placed, out_specs=P(None, "slab", "chan"), check_vma=False
    )
```

profile of v0, /device:TPU:0, one launch (start us, length us, event | category | flops | bytes accessed | tf_op | source)
XLA Modules:
  0.0 470.0 jit_solution(15943690405641390455)
XLA Ops:
  6.5 0.7 all-gather.2.cloned.1.call-update
  8.0 56.5 %all-gather.2.cloned.1.call-done = f32[2,256,2048]{2,1,0:T(8,128)} async-done(((f32[2,256,512]{2,1,0:T(8,128)}), f32[2,256,2048]{2,1,0:T(8,128)}) %all-gather.2.cloned.1.call-update) | async-done | bytes 4194320 | tf_op jit(solution)/shard_map/all_gather | solution.py:51
  64.5 2.5 fusion.2
  67.4 1.9 fusion.115
  69.4 2.3 subtract_bitcast_fusion.3
  71.7 2.6 fusion.37
  74.3 2.6 fusion.35
  76.9 2.8 subtract_bitcast_fusion.2
  79.7 1.2 copy.121
  81.0 2.6 add_bitcast_fusion.2
  83.5 1.2 copy.124
  85.0 12.2 %copy.125 = f32[2,2048,256]{2,0,1:T(2,128)} copy(f32[2,2048,256]{2,1,0:T(8,128)S(1)} %pad_maximum_fusion) | data formatting | bytes 8388608 | tf_op jit(solution)/shard_map/stack | solution.py:67
  97.3 5.1 %all-to-all-start = ((f32[2,2048,256]{2,0,1:T(2,128)}), f32[2,2048,256]{2,0,1:T(2,128)}, u32[]{:S(2)}, u32[]{:S(2)}) async-start(f32[2,2048,256]{2,0,1:T(2,128)} %copy.125), calls=%async_computation | async-start | bytes 8388608 | tf_op jit(solution)/shard_map/all_to_all | solution.py:68
  102.4 2.9 copy.115
  105.2 3.4 copy.116
  108.6 1.5 copy.117
  110.1 1.0 copy.118
  111.7 84.6 %all-to-all-done = f32[2,2048,256]{2,0,1:T(2,128)} async-done(((f32[2,2048,256]{2,0,1:T(2,128)}), f32[2,2048,256]{2,0,1:T(2,128)}, u32[]{:S(2)}, u32[]{:S(2)}) %all-to-all-start) | async-done | bytes 4194336 | tf_op jit(solution)/shard_map/all_to_all | solution.py:68
  196.4 2.5 copy.126
  198.9 1.7 fusion.277
  200.6 2.6 copy.127
  203.2 2.7 squeeze.28
  205.9 5.0 %fusion.112 = f32[16,256,128]{2,0,1:T(8,128)} fusion(f32[256,16,128]{2,1,0:T(8,128)} %squeeze.28), kind=kOutput, calls=%fused_computation.127 | convolution fusion | flops 100667136 | bytes 4194304 | tf_op jit(solution)/shard_map/uba,jb->uja/dot_general | solution.py:35
  210.9 3.3 fusion.121
  214.2 2.6 copy.128
  216.7 2.8 squeeze.29
  219.5 4.3 convolution_add_fusion
  223.9 2.4 subtract_bitcast_fusion.1
  226.4 2.5 fusion.27
  228.9 2.6 fusion.29
  231.5 3.0 fusion
  234.6 2.8 fusion.3
  237.4 2.4 fusion.68
  239.8 2.4 fusion.78
  242.1 2.4 convolution_subtract_fusion.1
  244.5 3.1 multiply_subtract_fusion.1
  247.7 2.9 fusion.21
  250.5 4.2 fusion.19
  254.7 4.3 subtract_bitcast_fusion
  259.0 2.7 stack.31
  261.8 6.2 %copy.137 = f32[1,256,2048]{1,0,2:T(1,128)} copy(f32[1,256,2048]{2,1,0:T(8,128)} %stack.31) | data formatting | bytes 4194304 | tf_op jit(solution)/shard_map/stack | solution.py:104
  268.0 5.8 %add_bitcast_fusion = f32[256,16,128]{2,1,0:T(8,128)} fusion(f32[16,256,128]{2,0,1:T(8,128)} %fusion.19, f32[256,16,128]{2,0,1:T(8,128)S(1)} %get-tuple-element.7), kind=kOutput, calls=%fused_computation.21 | convolution fusion | flops 101191680 | bytes 6291456 | tf_op jit(solution)/shard_map/uja,bj->uba/dot_general | solution.py:35
  273.8 1.7 stack.32
  275.5 3.7 copy.138
  279.1 6.7 %pad_maximum_fusion.1 = f32[2,256,2048]{1,0,2:T(2,128)} fusion(f32[1,256,2048]{1,0,2:T(1,128)} %copy.138, f32[1,256,2048]{1,0,2:T(1,128)} %copy.137), kind=kLoop, calls=%fused_computation.1 | loop fusion | flops 1048576 | bytes 8388608 | tf_op jit(solution)/shard_map/stack | solution.py:104
  285.9 4.6 all-to-all-start.1
  290.5 93.9 %all-to-all-done.1 = f32[2,256,2048]{1,0,2:T(2,128)} async-done(((f32[2,256,2048]{1,0,2:T(2,128)}), f32[2,256,2048]{1,0,2:T(2,128)}, u32[]{:S(2)}, u32[]{:S(2)}) %all-to-all-start.1) | async-done | bytes 4194336 | tf_op jit(solution)/shard_map/all_to_all | solution.py:105
  384.4 0.6 broadcast_in_dim.2
  385.0 3.2 all-to-all-start.3
  388.2 2.5 copy.139
  390.7 2.4 fusion.276
  393.1 1.9 copy.142
  395.1 4.5 fusion.13
  399.5 4.5 fusion.11
  404.0 2.1 copy.140
  406.2 5.0 %fusion.53 = f32[128,16,256]{2,0,1:T(8,128)S(1)} fusion(f32[128,16,256]{2,0,1:T(8,128)} %fusion.13, f32[128,16,256]{2,1,0:T(8,128)S(1)} %bitcast.149), kind=kOutput, calls=%fused_computation.68 | convolution fusion | flops 806060032 | bytes 6291456 | tf_op jit(solution)/shard_map/kjy,ak->ajy/dot_general | solution.py:32
  411.2 3.9 multiply_subtract_fusion
  415.1 2.9 fusion.5
  418.0 3.3 multiply_bitcast_fusion
  421.3 1.2 copy.148
  422.5 10.0 %copy.149 = f32[1,256,2048]{1,0,2:T(1,128)} copy(f32[1,256,2048]{1,2,0:T(8,128)S(1)} %bitcast.162) | data formatting | bytes 4194304 | tf_op jit(solution)/shard_map/div | solution.py:116
  432.5 4.2 all-to-all-start.2
  436.8 24.2 %all-to-all-done.2 = f32[1,256,2048]{1,0,2:T(1,128)S(1)} async-done(((f32[1,256,2048]{1,0,2:T(1,128)}), f32[1,256,2048]{1,0,2:T(1,128)S(1)}, u32[]{:S(2)}, u32[]{:S(2)}) %all-to-all-start.2) | async-done | bytes 2097184 | tf_op jit(solution)/shard_map/all_to_all | solution.py:124
  461.4 1.3 copy.151
  (23 shorter events, 1.4 us)
Async XLA Ops:
  6.5 58.0 %all-gather.2.cloned.1.call-start = ((), (), s32[]{:S(2)}) async-start(), calls=%async_computation.4 | async-start | bytes 5242880 | tf_op jit(solution)/shard_map/all_gather | solution.py:51
  97.3 99.1 %all-to-all-start = ((f32[2,2048,256]{2,0,1:T(2,128)}), f32[2,2048,256]{2,0,1:T(2,128)}, u32[]{:S(2)}, u32[]{:S(2)}) async-start(f32[2,2048,256]{2,0,1:T(2,128)} %copy.125), calls=%async_computation | async-start | bytes 8388608 | tf_op jit(solution)/shard_map/all_to_all | solution.py:68
  205.9 5.0 %copy-start.1 = (f32[256,16,128]{2,1,0:T(8,128)S(1)}, f32[256,16,128]{2,1,0:T(8,128)}, u32[]{:S(2)}) copy-start(f32[256,16,128]{2,1,0:T(8,128)} %squeeze.28) | copy-start | bytes 6291460
  210.9 3.3 copy-start.5
  219.5 4.4 copy-start
  219.5 4.4 copy-start.3
  228.9 2.6 copy-start.2
  285.9 98.5 %all-to-all-start.1 = ((f32[2,256,2048]{1,0,2:T(2,128)}), f32[2,256,2048]{1,0,2:T(2,128)}, u32[]{:S(2)}, u32[]{:S(2)}) async-start(f32[2,256,2048]{1,0,2:T(2,128)} %pad_maximum_fusion.1), calls=%async_computation.1 | async-start | bytes 8388608 | tf_op jit(solution)/shard_map/all_to_all | solution.py:105
  385.0 47.5 %all-to-all-start.3 = ((f32[1,1,4]{1,0,2:T(1,128)}), f32[1,1,4]{1,0,2:T(1,128)S(1)}, u32[]{:S(2)}, u32[]{:S(2)}) async-start(f32[1,1,4]{1,0,2:T(1,128)} %broadcast_in_dim.2), calls=%async_computation.3 | async-start | bytes 4096 | tf_op jit(solution)/shard_map/all_to_all | solution.py:125
  406.2 5.0 %copy-start.4 = (f32[128,16,256]{2,0,1:T(8,128)S(1)}, f32[128,16,256]{2,0,1:T(8,128)}, u32[]{:S(2)}) copy-start(f32[128,16,256]{2,0,1:T(8,128)} %fusion.11) | copy-start | bytes 6291460
  432.5 28.5 %all-to-all-start.2 = ((f32[1,256,2048]{1,0,2:T(1,128)}), f32[1,256,2048]{1,0,2:T(1,128)S(1)}, u32[]{:S(2)}, u32[]{:S(2)}) async-start(f32[1,256,2048]{1,0,2:T(1,128)} %copy.149), calls=%async_computation.2 | async-start | bytes 4194304 | tf_op jit(solution)/shard_map/all_to_all | solution.py:124
Sparse Core Ops, SparseCore 0:
  9.2 55.2 all-gather.1
where the time goes:
time: 480 us; the launch traced here: 470 us
  waiting for transfers between devices  260 us (54%)
  matrix products  92.3 us (19%)
  local copies, waits for them, and re-layouts  74.9 us (16%)
  starting transfers between devices  17 us (4%)
  between operations  15.5 us (3%)
  other arithmetic  10.3 us (2%)
    all_to_all x1, waiting for transfers between devices, local(): lax.all_to_all(outgoing_back, 'slab', split_axis=2, concat_axis=1, tiled=...  93.9 us
    all_to_all x1, waiting for transfers between devices, local(): lax.all_to_all(outgoing, 'slab', split_axis=1, concat_axis=2, tiled=True)  84.6 us
    all_gather x1, waiting for transfers between devices, local(): models = lax.all_gather(taylor_models, 'chan', axis=2, tiled=True)  56.5 us
    all_to_all x1, waiting for transfers between devices, local(): lax.all_to_all(stacked_res, 'chan', split_axis=2, concat_axis=0, tiled=True)  24.2 us
    dot_general x6, matrix products, complex_product(): jnp.einsum(formula, left_real, table_imag, precision=HIGHEST)  22.7 us
    dot_general x6, matrix products, complex_product(): jnp.einsum(formula, left_imag, table_real, precision=HIGHEST)  21.3 us
    dot_general x6, matrix products, complex_product(): jnp.einsum(formula, left_real, table_real, precision=HIGHEST)  20.6 us
    dot_general x6, matrix products, complex_product(): jnp.einsum(formula, left_imag, table_imag, precision=HIGHEST)  17.3 us
  transfers between devices with their start and end apart: 5, of which 4 were waited for; matrix products, arithmetic and copies ran while one was open for 11% of the time, Pallas kernels for 0%

commit v1 on v0

v1 whole, which is shorter than its diff:
```python
import functools
import math

import jax
import jax.numpy as jnp
import numpy as np
from jax import lax
from jax.experimental import pallas as pl
from jax.experimental.pallas import tpu as pltpu
from jax.sharding import PartitionSpec as P

INNER = 128


def split_bf16(x):
    high = x.astype(jnp.bfloat16)
    low = (x - high.astype(jnp.float32)).astype(jnp.bfloat16)
    return high, low


def table_pair(table):
    high = table.astype(np.float32).astype(jnp.bfloat16)
    low = (table - high.astype(np.float64)).astype(np.float32).astype(jnp.bfloat16)
    return np.stack([high, low])


@functools.cache
def tables(points):
    outer = points // INNER
    steps = np.arange(INNER)
    angle = 2.0 * np.pi * (np.outer(steps, steps) % INNER) / INNER
    cos, sin = np.cos(angle), np.sin(angle)
    forward = np.block([[cos, -sin], [sin, cos]])
    inverse = np.block([[cos, sin], [-sin, cos]])
    twist = 2.0 * np.pi * np.outer(np.arange(outer), steps) / points
    twist_table = np.stack([np.cos(twist), np.sin(twist)]).astype(np.float32)
    return table_pair(forward), table_pair(inverse), twist_table


def plus(x, y):
    return y if x is None else x if y is None else x + y


def minus(x, y):
    if y is None:
        return x
    return -y if x is None else x - y


def short_dft(values, sign):
    count = len(values)
    if count == 1:
        return values
    even = short_dft(values[0::2], sign)
    odd = short_dft(values[1::2], sign)
    half = count // 2
    out = [None] * count
    for k in range(half):
        (er, ei), (orr, oi) = even[k], odd[k]
        if k == 0:
            tr, ti = orr, oi
        elif 4 * k == count:
            tr, ti = (minus(None, oi), orr) if sign > 0 else (oi, minus(None, orr))
        else:
            c = math.cos(2.0 * math.pi * k / count)
            s = sign * math.sin(2.0 * math.pi * k / count)
            tr = minus(orr * c, None if oi is None else oi * s)
            ti = plus(orr * s, None if oi is None else oi * c)
        out[k] = (plus(er, tr), plus(ei, ti))
        out[k + half] = (minus(er, tr), minus(ei, ti))
    return out


def triple_dot(x, table_ref):
    high, low = split_bf16(x)
    dot = functools.partial(jnp.dot, preferred_element_type=jnp.float32)
    return dot(high, table_ref[0]) + dot(low, table_ref[0]) + dot(high, table_ref[1])


def rows_forward(x_ref, table_ref, twist_ref, out_ref):
    blocks, rows, width = x_ref.shape
    outer = blocks * width // INNER
    pieces = []
    for block in range(blocks):
        for start in range(0, width, INNER):
            pieces.append((x_ref[block, :, start : start + INNER], None))
    parts = short_dft(pieces, -1)
    turned = []
    for j in range(outer):
        re, im = parts[j]
        if im is None:
            im = jnp.zeros_like(re)
        c, s = twist_ref[0, j : j + 1, :], twist_ref[1, j : j + 1, :]
        turned.append(jnp.concatenate([re * c + im * s, im * c - re * s], axis=1))
    done = triple_dot(jnp.concatenate(turned, axis=0), table_ref)
    for j in range(outer):
        flipped = done[j * rows : (j + 1) * rows].T
        out_ref[0, j] = flipped[:INNER]
        out_ref[1, j] = flipped[INNER:]


def rows_inverse(x_ref, table_ref, twist_ref, out_ref):
    blocks, rows, width = out_ref.shape
    outer = x_ref.shape[1]
    scale = 1.0 / (outer * INNER)
    lines = [
        jnp.concatenate([x_ref[0, j], x_ref[1, j]], axis=0).T for j in range(outer)
    ]
    done = triple_dot(jnp.concatenate(lines, axis=0), table_ref)
    turned = []
    for j in range(outer):
        part = done[j * rows : (j + 1) * rows]
        re, im = part[:, :INNER], part[:, INNER:]
        c, s = twist_ref[0, j : j + 1, :] * scale, twist_ref[1, j : j + 1, :] * scale
        turned.append((re * c - im * s, im * c + re * s))
    result = short_dft(turned, 1)
    per_block = width // INNER
    for b in range(outer):
        start = (b % per_block) * INNER
        out_ref[b // per_block, :, start : start + INNER] = result[b][0]


def middle(
    damping_ref, x_ref, vis_ref, weight_ref, ahead_ref, back_ref, twist_ref, out_ref, work_ref, wide_ref
):
    _, outer, rows, _ = x_ref.shape
    scale = 1.0 / (outer * INNER)
    joined = jnp.concatenate(
        [x_ref[0].reshape(outer * rows, INNER), x_ref[1].reshape(outer * rows, INNER)], axis=1
    )
    work_ref[...] = triple_dot(joined, ahead_ref).reshape(outer, rows, 2 * INNER)
    wide_ref[0] = vis_ref[0, 0].astype(jnp.float32)
    wide_ref[1] = vis_ref[0, 1].astype(jnp.float32)
    wide_ref[2] = weight_ref[0].astype(jnp.float32)
    damping = damping_ref[0]

    def step(index, carry):
        at = pl.ds(pl.multiple_of(index * 8, 8), 8)
        values = []
        for b in range(outer):
            re, im = work_ref[b, at, :INNER], work_ref[b, at, INNER:]
            c, s = twist_ref[0, b : b + 1, :] * scale, twist_ref[1, b : b + 1, :] * scale
            values.append((re * c + im * s, im * c - re * s))
        spectrum = short_dft(values, -1)
        weighted = []
        for j in range(outer):
            lanes = slice(j * INNER, (j + 1) * INNER)
            weight = wide_ref[2, at, lanes]
            re = wide_ref[0, at, lanes] - weight * spectrum[j][0]
            im = wide_ref[1, at, lanes] - weight * spectrum[j][1]
            robust = 1.0 / (1.0 + damping * (re * re + im * im))
            weighted.append((robust * re, robust * im))
        inverse = short_dft(weighted, 1)
        for b in range(outer):
            re, im = inverse[b]
            c, s = twist_ref[0, b : b + 1, :], twist_ref[1, b : b + 1, :]
            work_ref[b, at, :INNER] = re * c - im * s
            work_ref[b, at, INNER:] = im * c + re * s
        return carry

    lax.fori_loop(0, rows // 8, step, 0)
    done = triple_dot(work_ref[...].reshape(outer * rows, 2 * INNER), back_ref)
    out_ref[0] = done[:, :INNER].reshape(outer, rows, INNER)
    out_ref[1] = done[:, INNER:].reshape(outer, rows, INNER)


VMEM = pl.BlockSpec(memory_space=pltpu.VMEM)


def local(chans, slabs, taylor_models, gridded_vis, uv_weight, freq_ratio, robust_scale):
    terms, rows, width = taylor_models.shape
    points = rows * slabs
    outer = points // INNER
    own_a, own_b, own_k = INNER // slabs, outer // chans, INNER // slabs
    ahead, back, twist = (jnp.asarray(t) for t in tables(points))
    f32 = jnp.float32
    offsets = lax.all_gather(freq_ratio, "chan", axis=0, tiled=True) - 1.0
    powers = jnp.stack([offsets**t for t in range(terms)])

    send = taylor_models.reshape(terms, own_a, chans, own_b, width).transpose(2, 0, 3, 1, 4)
    lines = terms * own_b * own_a
    got = lax.all_to_all(
        send.reshape(chans, lines, width), "chan", split_axis=0, concat_axis=0, tiled=True
    )
    part = pl.pallas_call(
        rows_forward,
        out_shape=jax.ShapeDtypeStruct((2, outer, INNER, lines), f32),
        in_specs=[VMEM] * 3,
        out_specs=VMEM,
        name="rows_forward",
    )(got, ahead, twist)

    send = part.reshape(2, outer, slabs, own_k, lines).transpose(2, 0, 1, 3, 4)
    got = lax.all_to_all(send, "slab", split_axis=0, concat_axis=0, tiled=True)
    got = got.reshape(slabs, 2, outer, own_k, terms, own_b, own_a)
    got = got.transpose(4, 1, 5, 3, 2, 0, 6).reshape(terms, 2, own_b, rows, INNER)
    mixed = got[0][None] + sum(
        powers[t][:, None, None, None, None] * got[t][None] for t in range(1, terms)
    )
    got = lax.all_to_all(mixed, "chan", split_axis=0, concat_axis=0, tiled=True)
    full = got.transpose(1, 0, 2, 3, 4).reshape(2, outer, rows, INNER)

    block = min(rows, 64)
    shape = (2, outer, block, INNER)
    result = pl.pallas_call(
        middle,
        grid=(rows // block,),
        out_shape=jax.ShapeDtypeStruct((2, outer, rows, INNER), f32),
        in_specs=[
            pl.BlockSpec(memory_space=pltpu.SMEM),
            pl.BlockSpec(shape, lambda i: (0, 0, i, 0)),
            pl.BlockSpec((1, 2, block, points), lambda i: (0, 0, i, 0)),
            pl.BlockSpec((1, block, points), lambda i: (0, i, 0)),
            pl.BlockSpec((2, 2 * INNER, 2 * INNER), lambda i: (0, 0, 0)),
            pl.BlockSpec((2, 2 * INNER, 2 * INNER), lambda i: (0, 0, 0)),
            pl.BlockSpec((2, outer, INNER), lambda i: (0, 0, 0)),
        ],
        out_specs=pl.BlockSpec(shape, lambda i: (0, 0, i, 0)),
        scratch_shapes=[
            pltpu.VMEM((outer, block, 2 * INNER), f32),
            pltpu.VMEM((3, block, points), f32),
        ],
        name="middle",
    )(robust_scale, full, gridded_vis, uv_weight, ahead, back, twist)

    send = result.reshape(2, chans, own_b, rows, INNER).transpose(1, 0, 2, 3, 4)
    got = lax.all_to_all(send, "chan", split_axis=0, concat_axis=0, tiled=True)
    summed = jnp.stack(
        [sum(powers[t, c] * got[c] for c in range(chans)) for t in range(terms)]
    )
    send = summed.reshape(terms, 2, own_b, own_k, outer, slabs, own_a)
    send = send.transpose(5, 1, 4, 3, 0, 2, 6).reshape(slabs, 2, outer, own_k, lines)
    got = lax.all_to_all(send, "slab", split_axis=0, concat_axis=0, tiled=True)
    part = got.transpose(1, 2, 0, 3, 4).reshape(2, outer, INNER, lines)
    image = pl.pallas_call(
        rows_inverse,
        out_shape=jax.ShapeDtypeStruct((chans, lines, width), f32),
        in_specs=[VMEM] * 3,
        out_specs=VMEM,
        name="rows_inverse",
    )(part, back, twist)
    got = lax.all_to_all(image, "chan", split_axis=0, concat_axis=0, tiled=True)
    got = got.reshape(chans, terms, own_b, own_a, width).transpose(1, 3, 0, 2, 4)
    return got.reshape(terms, rows, width)


def solution(mesh):
    placed = (
        P(None, "slab", "chan"),
        P("chan", None, "slab", None),
        P("chan", "slab", None),
        P("chan"),
        P("chan"),
    )
    body = functools.partial(local, mesh.shape["chan"], mesh.shape["slab"])
    return jax.shard_map(
        body, mesh=mesh, in_specs=placed, out_specs=P(None, "slab", "chan"), check_vma=False
    )
```

time: 480 us -> 382 us (0.80); the launches traced: 470 us -> 381 us
  waiting for transfers between devices: 260 us -> 131 us
  blocking collectives: 0 us -> 97.2 us
  matrix products: 92.3 us -> 0 us
  local copies, waits for them, and re-layouts: 74.9 us -> 99.6 us
  Pallas kernels: 0 us -> 22.3 us
  between operations: 15.5 us -> 1.39 us
    dot_general x28 -> x0, matrix products: 92.3 us -> none  [the longest x6 22.7 us: complex_product(): jnp.einsum(formula, left_real, table_imag, precision=HIGHEST)]
    all_to_all x0 -> x3, blocking collectives: none -> 88.8 us  [the longest x1 52.1 us: local(): got = lax.all_to_all(send, 'slab', split_axis=0, concat_axis=0, tiled=True)]
    all_to_all x4 -> x3, waiting for transfers between devices: 203 us -> 131 us  [the longest x1 46.6 us: local(): got = lax.all_to_all(mixed, 'chan', split_axis=0, concat_axis=0, tiled=True)]
    all_gather x1 -> x0, waiting for transfers between devices: 56.5 us -> none  [local(): models = lax.all_gather(taylor_models, 'chan', axis=2, tiled=True)]
    reshape x0 -> x8, local copies, waits for them, and re-layouts: none -> 52.7 us  [the longest x2 27.9 us: local(): got = got.reshape(slabs, 2, outer, own_k, terms, own_b, own_a)]
    pallas_call x0 -> x3, Pallas kernels: none -> 22.3 us  [the longest x1 14.5 us: local(): pl.pallas_call(middle, grid=(rows // block,), out_shape=jax.ShapeDtypeStr...]
    another operation x6 -> x2, local copies, waits for them, and re-layouts: 27.8 us -> 9.02 us  [local(): jnp.stack([sum((powers[t, c] * got[c] for c in range(chans))) for t in ra...]
    transpose x2 -> x4, local copies, waits for them, and re-layouts: 4.32 us -> 18.5 us  [the longest x1 11.6 us: local(): send.transpose(5, 1, 4, 3, 0, 2, 6).reshape(slabs, 2, outer, own_k, lines)]
  transfers between devices with their start and end apart: 5 -> 3, of which waited for: 4 -> 3; matrix products, arithmetic and copies ran while one was open for 11% -> 1% of each run, Pallas kernels for 0% -> 0%
where the time goes in v1:
time: 382 us; the launch traced here: 381 us
  waiting for transfers between devices  131 us (34%)
  local copies, waits for them, and re-layouts  99.6 us (26%)
  blocking collectives  97.2 us (25%)
  Pallas kernels  22.3 us (6%)
  starting transfers between devices  14.7 us (4%)
  other arithmetic  14.2 us (4%)
    all_to_all x1, blocking collectives, local(): got = lax.all_to_all(send, 'slab', split_axis=0, concat_axis=0, tiled=True)  52.1 us
    all_to_all x1, waiting for transfers between devices, local(): got = lax.all_to_all(mixed, 'chan', split_axis=0, concat_axis=0, tiled=True)  46.6 us
    all_to_all x1, waiting for transfers between devices, local(): got = lax.all_to_all(send, 'chan', split_axis=0, concat_axis=0, tiled=True)  46.3 us
    all_to_all x1, waiting for transfers between devices, local(): got = lax.all_to_all(send, 'slab', split_axis=0, concat_axis=0, tiled=True)  38.7 us
    reshape x2, local copies, waits for them, and re-layouts, local(): got = got.reshape(slabs, 2, outer, own_k, terms, own_b, own_a)  27.9 us
    all_to_all x1, blocking collectives, local(): lax.all_to_all(send.reshape(chans, lines, width), 'chan', split_axis=0, c...  19.2 us
    all_to_all x1, blocking collectives, local(): got = lax.all_to_all(image, 'chan', split_axis=0, concat_axis=0, tiled=True)  17.5 us
    pallas_call x1, Pallas kernels, local(): pl.pallas_call(middle, grid=(rows // block,), out_shape=jax.ShapeDtypeStr...  14.5 us
  transfers between devices with their start and end apart: 3, of which 3 were waited for; matrix products, arithmetic and copies ran while one was open for 1% of the time, Pallas kernels for 0%

profile of v1, /device:TPU:0, one launch (start us, length us, event | category | flops | bytes accessed | tf_op | source)
XLA Modules:
  0.0 380.9 jit_solution(7771755732430734092)
XLA Ops:
  0.0 1.5 reshape.39
  1.5 0.6 copy.22
  2.1 19.2 %all_to_all.30.x_ref = f32[4,128,512]{2,1,0:T(8,128)} all-to-all(f32[4,128,512]{2,1,0:T(8,128)S(1)} %bitcast.48), channel_id=1, replica_groups=mesh['chan'=4,'slab'=8] {'chan'}, dimensions={0} | all-to-all | bytes 2097152 | tf_op jit(solution)/shard_map/all_to_all | solution.py:182
  21.4 3.9 %rows_forward.1 = f32[2,16,128,128]{3,2,1,0:T(8,128)} custom-call(f32[4,128,512]{2,1,0:T(8,128)} %all_to_all.30.x_ref, bf16[2,256,256]{2,1,0:T(8,128)(2,1)} %constant.9.clone.table_ref.ahead_ref, f32[2,16,128]{2,1,0:T(8,128)} %constant.11.clone.twist_ref), custom_call_target="tpu_custom_call" | custom-call | tf_op jit(solution)/shard_map/rows_forward/pallas_call | solution.py:185
  25.3 0.0 copy-start
  25.3 3.1 copy.35
  28.5 4.9 %all-to-all-start.1 = ((f32[8,2,16,16,128]{4,3,2,1,0:T(8,128)}), f32[8,2,16,16,128]{4,3,2,1,0:T(8,128)S(1)}, u32[]{:S(2)}, u32[]{:S(2)}) async-start(f32[8,2,16,16,128]{4,3,2,1,0:T(8,128)} %bitcast.44), calls=%async_computation.1 | async-start | bytes 4194304 | tf_op jit(solution)/shard_map/all_to_all | solution.py:194
  34.0 0.0 copy-done
  34.0 0.6 dynamic-slice
  34.6 0.8 dynamic-update-slice
  35.4 8.3 %all-reduce = f32[4]{0:T(128)S(1)} all-reduce(f32[4]{0:T(128)S(1)} %dynamic-update-slice), channel_id=1, replica_groups=mesh['chan'=4,'slab'=8] {'chan'}, use_global_device_ids=true, to_apply=%add | all-reduce | flops 4 | bytes 32
  43.7 38.7 %all-to-all-done.1 = f32[8,2,16,16,128]{4,3,2,1,0:T(8,128)S(1)} async-done(((f32[8,2,16,16,128]{4,3,2,1,0:T(8,128)}), f32[8,2,16,16,128]{4,3,2,1,0:T(8,128)S(1)}, u32[]{:S(2)}, u32[]{:S(2)}) %all-to-all-start.1) | async-done | bytes 2097184 | tf_op jit(solution)/shard_map/all_to_all | solution.py:194
  82.4 12.6 %reshape.42 = f32[8,2,16,16,2,4,16]{6,5,4,3,2,1,0:T(4,128)} reshape(f32[8,2,16,16,128]{4,3,2,1,0:T(8,128)S(1)} %all-to-all-done.1) | data formatting | bytes 4194304 | tf_op jit(solution)/shard_map/reshape | solution.py:195
  95.0 15.2 %copy.33 = f32[8,2,16,16,2,4,16]{6,0,2,3,5,1,4:T(8,128)S(1)} copy(f32[8,2,16,16,2,4,16]{6,5,4,3,2,1,0:T(4,128)} %reshape.42) | data formatting | bytes 4194304 | tf_op jit(solution)/shard_map/reshape | solution.py:195
  110.3 6.3 %fusion.1 = (f32[1,2,4,16,16,8,16]{6,5,4,3,2,1,0:T(8,128)}, f32[1,2,4,16,16,8,16]{6,5,4,3,2,1,0:T(8,128)}) fusion(f32[2,2,4,16,16,8,16]{6,5,4,3,2,1,0:T(8,128)S(1)} %bitcast.40), kind=kLoop, calls=%fused_computation.9 | loop fusion | bytes 4194304 | tf_op jit(solution)/shard_map/slice | solution.py:197
  116.6 5.6 %mul.44 = f32[2,4,256,128]{3,2,1,0:T(8,128)S(1)} reshape(f32[1,2,4,16,16,8,16]{6,5,4,3,2,1,0:T(8,128)} %get-tuple-element.6) | data formatting | bytes 2097152 | tf_op jit(solution)/shard_map/mul | solution.py:198
  122.1 5.6 %add.35 = f32[2,4,256,128]{3,2,1,0:T(8,128)S(1)} reshape(f32[1,2,4,16,16,8,16]{6,5,4,3,2,1,0:T(8,128)} %get-tuple-element.5) | data formatting | bytes 2097152 | tf_op jit(solution)/shard_map/add | solution.py:197
  127.7 2.5 multiply_add_fusion
  130.3 5.0 %all-to-all-start.2 = ((f32[4,2,4,256,128]{4,3,2,1,0:T(8,128)}), f32[4,2,4,256,128]{4,3,2,1,0:T(8,128)}, u32[]{:S(2)}, u32[]{:S(2)}) async-start(f32[4,2,4,256,128]{4,3,2,1,0:T(8,128)} %multiply_add_fusion), calls=%async_computation.2 | async-start | bytes 8388608 | tf_op jit(solution)/shard_map/all_to_all | solution.py:200
  135.9 46.6 %all-to-all-done.2 = f32[4,2,4,256,128]{4,3,2,1,0:T(8,128)} async-done(((f32[4,2,4,256,128]{4,3,2,1,0:T(8,128)}), f32[4,2,4,256,128]{4,3,2,1,0:T(8,128)}, u32[]{:S(2)}, u32[]{:S(2)}) %all-to-all-start.2) | async-done | bytes 4194336 | tf_op jit(solution)/shard_map/all_to_all | solution.py:200
  182.5 4.6 %copy.25 = f32[2,4,4,256,128]{4,3,2,1,0:T(8,128)} copy(f32[2,4,4,256,128]{4,3,2,0,1:T(8,128)} %bitcast.6) | data formatting | bytes 8388608 | tf_op jit(solution)/shard_map/transpose | solution.py:201
  187.1 14.5 %middle.1 = f32[2,16,256,128]{3,2,1,0:T(8,128)} custom-call(f32[1]{0:T(128)S(6)} %copy.38.damping_ref, f32[2,16,256,128]{3,2,1,0:T(8,128)} %bitcast.41, bf16[1,2,256,2048]{3,2,1,0:T(8,128)(2,1)} %vis_ref.1, bf16[1,256,2048]{2,1,0:T(8,128)(2,1)} %weight_ref.1, bf16[2,256,256]{2,1,0:T(8,128)(2,1)} %constant.9.clone.table_ref.ahead_ref, ...), custom_call_target="tpu_custom_call" | custom-call | tf_op jit(solution)/shard_map/middle/pallas_call | solution.py:205
  201.6 4.6 %copy.34 = f32[2,4,4,256,128]{4,3,2,0,1:T(8,128)} copy(f32[2,4,4,256,128]{4,3,2,1,0:T(8,128)} %bitcast.42) | data formatting | bytes 8388608 | tf_op jit(solution)/shard_map/reshape | solution.py:226
  206.1 4.8 %all-to-all-start.3 = ((f32[4,2,4,256,128]{4,3,2,1,0:T(8,128)}), f32[4,2,4,256,128]{4,3,2,1,0:T(8,128)}, u32[]{:S(2)}, u32[]{:S(2)}) async-start(f32[4,2,4,256,128]{4,3,2,1,0:T(8,128)} %bitcast.43), calls=%async_computation.3 | async-start | bytes 8388608 | tf_op jit(solution)/shard_map/all_to_all | solution.py:227
  211.0 0.7 fusion.2
  211.6 46.3 %all-to-all-done.3 = f32[4,2,4,256,128]{4,3,2,1,0:T(8,128)} async-done(((f32[4,2,4,256,128]{4,3,2,1,0:T(8,128)}), f32[4,2,4,256,128]{4,3,2,1,0:T(8,128)}, u32[]{:S(2)}, u32[]{:S(2)}) %all-to-all-start.3) | async-done | bytes 4194336 | tf_op jit(solution)/shard_map/all_to_all | solution.py:227
  257.9 5.1 %add_add_fusion = (f32[1,2,4,256,128]{4,3,2,1,0:T(8,128)S(1)}, f32[1,2,4,256,128]{4,3,2,1,0:T(8,128)S(1)}) fusion(f32[4,2,4,256,128]{4,3,2,1,0:T(8,128)} %all-to-all-done.3, f32[]{:T(128)} %bitcast.14, f32[]{:T(128)} %bitcast.13, f32[]{:T(128)} %bitcast.12, f32[]{:T(128)} %bitcast.11), kind=kLoop, calls=%fused_computation.6 | loop fusion | flops 2621440 | bytes 6291472 | tf_op jit(solution)/shard_map/add | solution.py:229
  263.0 4.5 %stack.14 = f32[1,2,4,16,16,8,16]{6,5,4,3,2,1,0:T(8,128)} reshape(f32[1,2,4,256,128]{4,3,2,1,0:T(8,128)S(1)} %get-tuple-element.8) | data formatting | bytes 2097152 | tf_op jit(solution)/shard_map/stack | solution.py:228
  267.6 4.5 %stack.12 = f32[1,2,4,16,16,8,16]{6,5,4,3,2,1,0:T(8,128)} reshape(f32[1,2,4,256,128]{4,3,2,1,0:T(8,128)S(1)} %get-tuple-element.7) | data formatting | bytes 2097152 | tf_op jit(solution)/shard_map/stack | solution.py:228
  272.0 6.6 %maximum_bitcast_fusion = f32[8,2,16,16,2,4,16]{6,0,2,3,5,1,4:T(8,128)S(1)} fusion(f32[1,2,4,16,16,8,16]{6,5,4,3,2,1,0:T(8,128)} %stack.14, f32[1,2,4,16,16,8,16]{6,5,4,3,2,1,0:T(8,128)} %stack.12), kind=kLoop, calls=%fused_computation | loop fusion | flops 524288 | bytes 4194304 | tf_op jit(solution)/shard_map/transpose | solution.py:232
  278.6 11.6 %copy.27 = f32[8,2,16,16,2,4,16]{6,5,4,3,2,1,0:T(4,128)} copy(f32[8,2,16,16,2,4,16]{6,0,2,3,5,1,4:T(8,128)S(1)} %maximum_bitcast_fusion) | data formatting | bytes 4194304 | tf_op jit(solution)/shard_map/transpose | solution.py:232
  290.2 13.6 %reshape.45 = f32[8,2,16,16,128]{4,3,2,1,0:T(8,128)S(1)} reshape(f32[8,2,16,16,2,4,16]{6,5,4,3,2,1,0:T(4,128)} %copy.27) | data formatting | bytes 4194304 | tf_op jit(solution)/shard_map/reshape | solution.py:232
  303.8 52.1 %all_to_all.31 = f32[8,2,16,16,128]{4,3,2,1,0:T(8,128)S(1)} all-to-all(f32[8,2,16,16,128]{4,3,2,1,0:T(8,128)S(1)} %reshape.45), channel_id=1, replica_groups=mesh['chan'=4,'slab'=8] {'slab'}, dimensions={0} | all-to-all | bytes 4194304 | tf_op jit(solution)/shard_map/all_to_all | solution.py:233
  355.9 1.6 copy.28
  357.5 3.9 %rows_inverse.1 = f32[4,128,512]{2,1,0:T(8,128)} custom-call(f32[2,16,128,128]{3,2,1,0:T(8,128)} %bitcast.45, bf16[2,256,256]{2,1,0:T(8,128)(2,1)} %constant.10.clone.back_ref.table_ref, f32[2,16,128]{2,1,0:T(8,128)} %constant.11.clone.twist_ref), custom_call_target="tpu_custom_call" | custom-call | tf_op jit(solution)/shard_map/rows_inverse/pallas_call | solution.py:235
  361.4 17.5 %all_to_all.32 = f32[4,128,512]{2,1,0:T(8,128)S(1)} all-to-all(f32[4,128,512]{2,1,0:T(8,128)} %rows_inverse.1), channel_id=1, replica_groups=mesh['chan'=4,'slab'=8] {'chan'}, dimensions={0} | all-to-all | bytes 2097152 | tf_op jit(solution)/shard_map/all_to_all | solution.py:242
  378.9 0.7 copy.29
  379.6 1.3 reshape.48
  (2 shorter events, 0.0 us)
Async XLA Ops:
  25.3 8.7 %copy-start = (u32[32]{0:T(128)S(1)}, u32[32]{0:T(128)}, u32[]{:S(2)}) copy-start(u32[32]{0:T(128)} %constant.18) | copy-start | bytes 388
  28.5 53.9 %all-to-all-start.1 = ((f32[8,2,16,16,128]{4,3,2,1,0:T(8,128)}), f32[8,2,16,16,128]{4,3,2,1,0:T(8,128)S(1)}, u32[]{:S(2)}, u32[]{:S(2)}) async-start(f32[8,2,16,16,128]{4,3,2,1,0:T(8,128)} %bitcast.44), calls=%async_computation.1 | async-start | bytes 4194304 | tf_op jit(solution)/shard_map/all_to_all | solution.py:194
  130.3 52.2 %all-to-all-start.2 = ((f32[4,2,4,256,128]{4,3,2,1,0:T(8,128)}), f32[4,2,4,256,128]{4,3,2,1,0:T(8,128)}, u32[]{:S(2)}, u32[]{:S(2)}) async-start(f32[4,2,4,256,128]{4,3,2,1,0:T(8,128)} %multiply_add_fusion), calls=%async_computation.2 | async-start | bytes 8388608 | tf_op jit(solution)/shard_map/all_to_all | solution.py:200
  206.1 51.8 %all-to-all-start.3 = ((f32[4,2,4,256,128]{4,3,2,1,0:T(8,128)}), f32[4,2,4,256,128]{4,3,2,1,0:T(8,128)}, u32[]{:S(2)}, u32[]{:S(2)}) async-start(f32[4,2,4,256,128]{4,3,2,1,0:T(8,128)} %bitcast.43), calls=%async_computation.3 | async-start | bytes 8388608 | tf_op jit(solution)/shard_map/all_to_all | solution.py:227

commit v2 on v1

--- a/solution.py
+++ b/solution.py
@@ -10,6 +10,7 @@
 from jax.sharding import PartitionSpec as P
 
 INNER = 128
+CHUNKS = 2
 
 
 def split_bf16(x):
@@ -77,7 +78,7 @@
     return dot(high, table_ref[0]) + dot(low, table_ref[0]) + dot(high, table_ref[1])
 
 
-def rows_forward(x_ref, table_ref, twist_ref, out_ref):
+def rows_forward(x_ref, table_ref, twist_ref, *out_refs):
     blocks, rows, width = x_ref.shape
     outer = blocks * width // INNER
     pieces = []
@@ -93,19 +94,31 @@
         c, s = twist_ref[0, j : j + 1, :], twist_ref[1, j : j + 1, :]
         turned.append(jnp.concatenate([re * c + im * s, im * c - re * s], axis=1))
     done = triple_dot(jnp.concatenate(turned, axis=0), table_ref)
+    slabs, _, per_chunk = out_refs[0].shape[:3]
+    own_k = per_chunk * len(out_refs)
     for j in range(outer):
         flipped = done[j * rows : (j + 1) * rows].T
-        out_ref[0, j] = flipped[:INNER]
-        out_ref[1, j] = flipped[INNER:]
-
-
-def rows_inverse(x_ref, table_ref, twist_ref, out_ref):
+        for slab in range(slabs):
+            for chunk, out_ref in enumerate(out_refs):
+                for part in range(2):
+                    start = part * INNER + slab * own_k + chunk * per_chunk
+                    out_ref[slab, part, :, j, :] = flipped[start : start + per_chunk]
+
+
+def rows_inverse(table_ref, twist_ref, *refs):
+    x_refs, out_ref = refs[:-1], refs[-1]
     blocks, rows, width = out_ref.shape
-    outer = x_ref.shape[1]
+    slabs, _, _, outer, _ = x_refs[0].shape
     scale = 1.0 / (outer * INNER)
-    lines = [
-        jnp.concatenate([x_ref[0, j], x_ref[1, j]], axis=0).T for j in range(outer)
-    ]
+    lines = []
+    for j in range(outer):
+        line = [
+            x_ref[slab, part, :, j, :]
+            for part in range(2)
+            for slab in range(slabs)
+            for x_ref in x_refs
+        ]
+        lines.append(jnp.concatenate(line, axis=0).T)
     done = triple_dot(jnp.concatenate(lines, axis=0), table_ref)
     turned = []
     for j in range(outer):
@@ -120,13 +133,49 @@
         out_ref[b // per_block, :, start : start + INNER] = result[b][0]
 
 
+def mix(power_ref, x_ref, out_ref):
+    slabs, _, _, lines = x_ref.shape
+    chans, _, own_b, _, _ = out_ref.shape
+    terms = power_ref.shape[0]
+    own_a = lines // (terms * own_b)
+    x = [x_ref[slab, 0] for slab in range(slabs)]
+    for b in range(own_b):
+        by_term = []
+        for t in range(terms):
+            start = (t * own_b + b) * own_a
+            by_term.append(jnp.concatenate([p[:, start : start + own_a] for p in x], axis=1))
+        for c in range(chans):
+            total = by_term[0]
+            for t in range(1, terms):
+                total = total + power_ref[t, c] * by_term[t]
+            out_ref[c, 0, b] = total
+
+
+def gather_terms(power_ref, x_ref, out_ref):
+    chans, _, own_b, _, _ = x_ref.shape
+    slabs, _, _, lines = out_ref.shape
+    terms = power_ref.shape[0]
+    own_a = lines // (terms * own_b)
+    sums = []
+    for t in range(terms):
+        for b in range(own_b):
+            total = x_ref[0, 0, b] if t == 0 else power_ref[t, 0] * x_ref[0, 0, b]
+            for c in range(1, chans):
+                total = total + (x_ref[c, 0, b] if t == 0 else power_ref[t, c] * x_ref[c, 0, b])
+            sums.append(total)
+    for slab in range(slabs):
+        lanes = slice(slab * own_a, (slab + 1) * own_a)
+        out_ref[slab, 0] = jnp.concatenate([total[:, lanes] for total in sums], axis=1)
+
+
 def middle(
     damping_ref, x_ref, vis_ref, weight_ref, ahead_ref, back_ref, twist_ref, out_ref, work_ref, wide_ref
 ):
-    _, outer, rows, _ = x_ref.shape
+    chans, _, own_b, rows, _ = x_ref.shape
+    outer = chans * own_b
     scale = 1.0 / (outer * INNER)
     joined = jnp.concatenate(
-        [x_ref[0].reshape(outer * rows, INNER), x_ref[1].reshape(outer * rows, INNER)], axis=1
+        [x_ref[:, part].reshape(outer * rows, INNER) for part in range(2)], axis=1
     )
     work_ref[...] = triple_dot(joined, ahead_ref).reshape(outer, rows, 2 * INNER)
     wide_ref[0] = vis_ref[0, 0].astype(jnp.float32)
@@ -160,8 +209,8 @@
 
     lax.fori_loop(0, rows // 8, step, 0)
     done = triple_dot(work_ref[...].reshape(outer * rows, 2 * INNER), back_ref)
-    out_ref[0] = done[:, :INNER].reshape(outer, rows, INNER)
-    out_ref[1] = done[:, INNER:].reshape(outer, rows, INNER)
+    out_ref[:, 0] = done[:, :INNER].reshape(chans, own_b, rows, INNER)
+    out_ref[:, 1] = done[:, INNER:].reshape(chans, own_b, rows, INNER)
 
 
 VMEM = pl.BlockSpec(memory_space=pltpu.VMEM)
@@ -182,63 +231,84 @@
     got = lax.all_to_all(
         send.reshape(chans, lines, width), "chan", split_axis=0, concat_axis=0, tiled=True
     )
-    part = pl.pallas_call(
+    chunks = CHUNKS if own_k % CHUNKS == 0 else 1
+    own_u = rows // chunks
+    parts = pl.pallas_call(
         rows_forward,
-        out_shape=jax.ShapeDtypeStruct((2, outer, INNER, lines), f32),
+        out_shape=[
+            jax.ShapeDtypeStruct((slabs, 2, own_k // chunks, outer, lines), f32)
+            for _ in range(chunks)
+        ],
         in_specs=[VMEM] * 3,
-        out_specs=VMEM,
+        out_specs=[VMEM] * chunks,
         name="rows_forward",
     )(got, ahead, twist)
 
-    send = part.reshape(2, outer, slabs, own_k, lines).transpose(2, 0, 1, 3, 4)
-    got = lax.all_to_all(send, "slab", split_axis=0, concat_axis=0, tiled=True)
-    got = got.reshape(slabs, 2, outer, own_k, terms, own_b, own_a)
-    got = got.transpose(4, 1, 5, 3, 2, 0, 6).reshape(terms, 2, own_b, rows, INNER)
-    mixed = got[0][None] + sum(
-        powers[t][:, None, None, None, None] * got[t][None] for t in range(1, terms)
-    )
-    got = lax.all_to_all(mixed, "chan", split_axis=0, concat_axis=0, tiled=True)
-    full = got.transpose(1, 0, 2, 3, 4).reshape(2, outer, rows, INNER)
-
-    block = min(rows, 64)
-    shape = (2, outer, block, INNER)
-    result = pl.pallas_call(
-        middle,
-        grid=(rows // block,),
-        out_shape=jax.ShapeDtypeStruct((2, outer, rows, INNER), f32),
-        in_specs=[
-            pl.BlockSpec(memory_space=pltpu.SMEM),
-            pl.BlockSpec(shape, lambda i: (0, 0, i, 0)),
-            pl.BlockSpec((1, 2, block, points), lambda i: (0, 0, i, 0)),
-            pl.BlockSpec((1, block, points), lambda i: (0, i, 0)),
-            pl.BlockSpec((2, 2 * INNER, 2 * INNER), lambda i: (0, 0, 0)),
-            pl.BlockSpec((2, 2 * INNER, 2 * INNER), lambda i: (0, 0, 0)),
-            pl.BlockSpec((2, outer, INNER), lambda i: (0, 0, 0)),
-        ],
-        out_specs=pl.BlockSpec(shape, lambda i: (0, 0, i, 0)),
-        scratch_shapes=[
-            pltpu.VMEM((outer, block, 2 * INNER), f32),
-            pltpu.VMEM((3, block, points), f32),
-        ],
-        name="middle",
-    )(robust_scale, full, gridded_vis, uv_weight, ahead, back, twist)
-
-    send = result.reshape(2, chans, own_b, rows, INNER).transpose(1, 0, 2, 3, 4)
-    got = lax.all_to_all(send, "chan", split_axis=0, concat_axis=0, tiled=True)
-    summed = jnp.stack(
-        [sum(powers[t, c] * got[c] for c in range(chans)) for t in range(terms)]
-    )
-    send = summed.reshape(terms, 2, own_b, own_k, outer, slabs, own_a)
-    send = send.transpose(5, 1, 4, 3, 0, 2, 6).reshape(slabs, 2, outer, own_k, lines)
-    got = lax.all_to_all(send, "slab", split_axis=0, concat_axis=0, tiled=True)
-    part = got.transpose(1, 2, 0, 3, 4).reshape(2, outer, INNER, lines)
+    exchange = functools.partial(lax.all_to_all, split_axis=0, concat_axis=0, tiled=True)
+    smem = pl.BlockSpec(memory_space=pltpu.SMEM)
+    step = min(own_u, 64)
+    by_chan = (chans, 2, own_b, own_u, INNER)
+    by_slab = (slabs, 2, own_u, lines)
+    chan_spec = pl.BlockSpec((chans, 1, own_b, step, INNER), lambda p, i: (0, p, 0, i, 0))
+    slab_spec = pl.BlockSpec((slabs, 1, step, lines), lambda p, i: (0, p, i, 0))
+    block = min(own_u, 64)
+    whole_spec = pl.BlockSpec((chans, 2, own_b, block, INNER), lambda i: (0, 0, 0, i, 0))
+
+    arrived = [exchange(part.reshape(by_slab), "slab") for part in parts]
+    full = []
+    for got in arrived:
+        mixed = pl.pallas_call(
+            mix,
+            grid=(2, own_u // step),
+            out_shape=jax.ShapeDtypeStruct(by_chan, f32),
+            in_specs=[smem, slab_spec],
+            out_specs=chan_spec,
+            name="mix",
+        )(powers, got)
+        full.append(exchange(mixed, "chan"))
+
+    back_parts = []
+    for chunk, got in enumerate(full):
+        first = chunk * (own_u // block)
+        result = pl.pallas_call(
+            middle,
+            grid=(own_u // block,),
+            out_shape=jax.ShapeDtypeStruct(by_chan, f32),
+            in_specs=[
+                smem,
+                whole_spec,
+                pl.BlockSpec((1, 2, block, points), lambda i, first=first: (0, 0, i + first, 0)),
+                pl.BlockSpec((1, block, points), lambda i, first=first: (0, i + first, 0)),
+                pl.BlockSpec((2, 2 * INNER, 2 * INNER), lambda i: (0, 0, 0)),
+                pl.BlockSpec((2, 2 * INNER, 2 * INNER), lambda i: (0, 0, 0)),
+                pl.BlockSpec((2, outer, INNER), lambda i: (0, 0, 0)),
+            ],
+            out_specs=whole_spec,
+            scratch_shapes=[
+                pltpu.VMEM((outer, block, 2 * INNER), f32),
+                pltpu.VMEM((3, block, points), f32),
+            ],
+            name="middle",
+        )(robust_scale, got, gridded_vis, uv_weight, ahead, back, twist)
+        got = exchange(result, "chan")
+        summed = pl.pallas_call(
+            gather_terms,
+            grid=(2, own_u // step),
+            out_shape=jax.ShapeDtypeStruct(by_slab, f32),
+            in_specs=[smem, chan_spec],
+            out_specs=slab_spec,
+            name="gather_terms",
+        )(powers, got)
+        got = exchange(summed, "slab")
+        back_parts.append(got.reshape(slabs, 2, own_k // chunks, outer, lines))
+
     image = pl.pallas_call(
         rows_inverse,
         out_shape=jax.ShapeDtypeStruct((chans, lines, width), f32),
-        in_specs=[VMEM] * 3,
+        in_specs=[VMEM] * (2 + chunks),
         out_specs=VMEM,
         name="rows_inverse",
-    )(part, back, twist)
+    )(back, twist, *back_parts)
     got = lax.all_to_all(image, "chan", split_axis=0, concat_axis=0, tiled=True)
     got = got.reshape(chans, terms, own_b, own_a, width).transpose(1, 3, 0, 2, 4)
     return got.reshape(terms, rows, width)

time: 382 us -> 291 us (0.76)
  local copies, waits for them, and re-layouts: 99.6 us -> 10.1 us
  waiting for transfers between devices: 131 us -> 103 us
  Pallas kernels: 22.3 us -> 45.4 us
  other arithmetic: 14.2 us -> 0.01 us
  blocking collectives: 97.2 us -> 108 us
  starting transfers between devices: 14.7 us -> 22.4 us
    reshape x5 -> x0, local copies, waits for them, and re-layouts: 49.2 us -> none  [the longest x2 27.9 us: local(): got = got.reshape(slabs, 2, outer, own_k, terms, own_b, own_a)]
    all_to_all x3 -> x6, waiting for transfers between devices: 131 us -> 103 us  [the longest x2 35.5 us: local(): got = exchange(result, 'chan')]
    pallas_call x2 -> x7, Pallas kernels: 18.4 us -> 40.8 us  [the longest x2 17.1 us: local(): pl.pallas_call(middle, grid=(own_u // block,), out_shape=jax.ShapeDtypeSt...]
    transpose x3 -> x0, local copies, waits for them, and re-layouts: 17.8 us -> none  [the longest x1 11.6 us: local(): send.transpose(5, 1, 4, 3, 0, 2, 6).reshape(slabs, 2, outer, own_k, lines)]
    all_to_all x1 -> x2, blocking collectives: 52.1 us -> 62.5 us  [the longest x1 31.7 us: local(): arrived = [exchange(part.reshape(by_slab), 'slab') for part in parts]]
    another operation x2 -> x1, local copies, waits for them, and re-layouts: 9.02 us -> 0.58 us  [local(): powers = jnp.stack([offsets ** t for t in range(terms)])]
    all_to_all x3 -> x6, starting transfers between devices: 14.7 us -> 22.4 us  [the longest x2 8.05 us: local(): got = exchange(result, 'chan')]
    add x2 -> x0, other arithmetic: 7.66 us -> none  [the longest x1 5.11 us: local(): sum((powers[t, c] * got[c] for c in range(chans)))]
  transfers between devices with their start and end apart: 3 -> 6, of which waited for: 3 -> 6; matrix products, arithmetic and copies ran while one was open for 1% -> 1% of each run, Pallas kernels for 0% -> 12%
where the time goes in v2:
time: 291 us; the launch traced here: 290 us
  blocking collectives  108 us (37%)
  waiting for transfers between devices  103 us (35%)
  Pallas kernels  45.4 us (16%)
  starting transfers between devices  22.4 us (8%)
  local copies, waits for them, and re-layouts  10.1 us (3%)
    all_to_all x2, waiting for transfers between devices, local(): got = exchange(result, 'chan')  35.5 us
    all_to_all x2, waiting for transfers between devices, local(): full.append(exchange(mixed, 'chan'))  35.3 us
    all_to_all x1, blocking collectives, local(): arrived = [exchange(part.reshape(by_slab), 'slab') for part in parts]  31.7 us
    all_to_all x1, blocking collectives, local(): got = exchange(summed, 'slab')  30.8 us
    all_to_all x1, waiting for transfers between devices, local(): got = exchange(summed, 'slab')  21.8 us
    all_to_all x1, blocking collectives, local(): lax.all_to_all(send.reshape(chans, lines, width), 'chan', split_axis=0, c...  19.2 us
    all_to_all x1, blocking collectives, local(): got = lax.all_to_all(image, 'chan', split_axis=0, concat_axis=0, tiled=True)  17.5 us
    pallas_call x2, Pallas kernels, local(): pl.pallas_call(middle, grid=(own_u // block,), out_shape=jax.ShapeDtypeSt...  17.1 us
  transfers between devices with their start and end apart: 6, of which 6 were waited for; matrix products, arithmetic and copies ran while one was open for 1% of the time, Pallas kernels for 12%

profile of v2, /device:TPU:0, one launch (start us, length us, event | category | flops | bytes accessed | tf_op | source)
XLA Modules:
  0.0 290.2 jit_solution(7101315813753666093)
XLA Ops:
  0.0 1.5 reshape.24
  1.5 0.6 copy.9
  2.1 19.2 %all_to_all.50.x_ref = f32[4,128,512]{2,1,0:T(8,128)} all-to-all(f32[4,128,512]{2,1,0:T(8,128)S(1)} %bitcast.15), channel_id=1, replica_groups=mesh['chan'=4,'slab'=8] {'chan'}, dimensions={0} | all-to-all | bytes 2097152 | tf_op jit(solution)/shard_map/all_to_all | solution.py:231
  21.4 4.8 %rows_forward.1 = (f32[8,2,8,16,128]{4,3,2,1,0:T(8,128)}, f32[8,2,8,16,128]{4,3,2,1,0:T(8,128)}) custom-call(f32[4,128,512]{2,1,0:T(8,128)} %all_to_all.50.x_ref, bf16[2,256,256]{2,1,0:T(8,128)(2,1)} %constant.11.clone.table_ref.ahead_ref, f32[2,16,128]{2,1,0:T(8,128)} %constant.13.clone.twist_ref), custom_call_target="tpu_custom_call" | custom-call | tf_op jit(solution)/shard_map/rows_forward/pallas_call | solution.py:236
  26.2 0.0 copy-start.5
  26.2 31.7 %all_to_all.51.x_ref = f32[8,2,128,128]{3,2,1,0:T(8,128)} all-to-all(f32[8,2,128,128]{3,2,1,0:T(8,128)} %bitcast.17), channel_id=1, replica_groups=mesh['chan'=4,'slab'=8] {'slab'}, dimensions={0} | all-to-all | bytes 2097152 | tf_op jit(solution)/shard_map/all_to_all | solution.py:257
  57.9 3.6 %all-to-all-start.5 = ((f32[8,2,128,128]{3,2,1,0:T(8,128)}), f32[8,2,128,128]{3,2,1,0:T(8,128)S(1)}, u32[]{:S(2)}, u32[]{:S(2)}) async-start(f32[8,2,128,128]{3,2,1,0:T(8,128)} %bitcast.6), calls=%async_computation.5 | async-start | bytes 2097152 | tf_op jit(solution)/shard_map/all_to_all | solution.py:257
  62.1 0.0 copy-done.5
  62.1 0.6 dynamic-slice
  62.7 0.8 dynamic-update-slice
  63.5 8.3 %all-reduce.1 = f32[4]{0:T(128)S(1)} all-reduce(f32[4]{0:T(128)S(1)} %dynamic-update-slice), channel_id=1, replica_groups=mesh['chan'=4,'slab'=8] {'chan'}, use_global_device_ids=true, to_apply=%add.1 | all-reduce | flops 4 | bytes 32
  71.8 0.6 stack.7.power_ref
  72.4 4.8 %mix.2 = f32[4,2,4,128,128]{4,3,2,1,0:T(8,128)} custom-call(f32[2,4]{1,0:T(2,128)} %stack.7.power_ref, f32[8,2,128,128]{3,2,1,0:T(8,128)} %all_to_all.51.x_ref), custom_call_target="tpu_custom_call" | custom-call | tf_op jit(solution)/shard_map/mix/pallas_call | solution.py:260
  77.2 10.8 %all-to-all-done.5.x_ref = f32[8,2,128,128]{3,2,1,0:T(8,128)S(1)} async-done(((f32[8,2,128,128]{3,2,1,0:T(8,128)}), f32[8,2,128,128]{3,2,1,0:T(8,128)S(1)}, u32[]{:S(2)}, u32[]{:S(2)}) %all-to-all-start.5) | async-done | bytes 1048608 | tf_op jit(solution)/shard_map/all_to_all | solution.py:257
  87.9 0.0 copy-start.3
  87.9 3.6 %all-to-all-start.2 = ((f32[4,2,4,128,128]{4,3,2,1,0:T(8,128)}), f32[4,2,4,128,128]{4,3,2,1,0:T(8,128)S(1)}, u32[]{:S(2)}, u32[]{:S(2)}) async-start(f32[4,2,4,128,128]{4,3,2,1,0:T(8,128)} %mix.2), calls=%async_computation.2 | async-start | bytes 4194304 | tf_op jit(solution)/shard_map/all_to_all | solution.py:268
  91.6 0.0 copy-done.3
  91.6 4.7 %mix.3 = f32[4,2,4,128,128]{4,3,2,1,0:T(8,128)} custom-call(f32[2,4]{1,0:T(2,128)} %stack.7.power_ref, f32[8,2,128,128]{3,2,1,0:T(8,128)} %copy-done.3), custom_call_target="tpu_custom_call" | custom-call | tf_op jit(solution)/shard_map/mix/pallas_call | solution.py:260
  96.3 20.1 %all-to-all-done.2.x_ref = f32[4,2,4,128,128]{4,3,2,1,0:T(8,128)S(1)} async-done(((f32[4,2,4,128,128]{4,3,2,1,0:T(8,128)}), f32[4,2,4,128,128]{4,3,2,1,0:T(8,128)S(1)}, u32[]{:S(2)}, u32[]{:S(2)}) %all-to-all-start.2) | async-done | bytes 2097184 | tf_op jit(solution)/shard_map/all_to_all | solution.py:268
  116.4 0.0 copy-start.2
  116.4 1.4 copy-done.2
  117.7 3.6 %all-to-all-start.6 = ((f32[4,2,4,128,128]{4,3,2,1,0:T(8,128)}), f32[4,2,4,128,128]{4,3,2,1,0:T(8,128)S(1)}, u32[]{:S(2)}, u32[]{:S(2)}) async-start(f32[4,2,4,128,128]{4,3,2,1,0:T(8,128)} %mix.3), calls=%async_computation.6 | async-start | bytes 4194304 | tf_op jit(solution)/shard_map/all_to_all | solution.py:268
  122.0 8.5 %middle.2 = f32[4,2,4,128,128]{4,3,2,1,0:T(8,128)} custom-call(f32[1]{0:T(128)S(6)} %copy.13.damping_ref, f32[4,2,4,128,128]{4,3,2,1,0:T(8,128)} %copy-done.2, bf16[1,2,256,2048]{3,2,1,0:T(8,128)(2,1)} %vis_ref.3, bf16[1,256,2048]{2,1,0:T(8,128)(2,1)} %weight_ref.3, bf16[2,256,256]{2,1,0:T(8,128)(2,1)} %constant.11.clone.table_ref.ahead_ref, ...), custom_call_target="tpu_custom_call" | custom-call | tf_op jit(solution)/shard_map/middle/pallas_call | solution.py:273
  130.5 15.2 %all-to-all-done.6.x_ref = f32[4,2,4,128,128]{4,3,2,1,0:T(8,128)S(1)} async-done(((f32[4,2,4,128,128]{4,3,2,1,0:T(8,128)}), f32[4,2,4,128,128]{4,3,2,1,0:T(8,128)S(1)}, u32[]{:S(2)}, u32[]{:S(2)}) %all-to-all-start.6) | async-done | bytes 2097184 | tf_op jit(solution)/shard_map/all_to_all | solution.py:268
  145.7 0.0 copy-start.1
  145.7 1.4 copy-done.1
  147.1 3.6 %all-to-all-start.3 = ((f32[4,2,4,128,128]{4,3,2,1,0:T(8,128)}), f32[4,2,4,128,128]{4,3,2,1,0:T(8,128)S(1)}, u32[]{:S(2)}, u32[]{:S(2)}) async-start(f32[4,2,4,128,128]{4,3,2,1,0:T(8,128)} %middle.2), calls=%async_computation.3 | async-start | bytes 4194304 | tf_op jit(solution)/shard_map/all_to_all | solution.py:293
  150.7 8.6 %middle.3 = f32[4,2,4,128,128]{4,3,2,1,0:T(8,128)} custom-call(f32[1]{0:T(128)S(6)} %copy.13.damping_ref, f32[4,2,4,128,128]{4,3,2,1,0:T(8,128)} %copy-done.1, bf16[1,2,256,2048]{3,2,1,0:T(8,128)(2,1)} %vis_ref.3, bf16[1,256,2048]{2,1,0:T(8,128)(2,1)} %weight_ref.3, bf16[2,256,256]{2,1,0:T(8,128)(2,1)} %constant.11.clone.table_ref.ahead_ref, ...), custom_call_target="tpu_custom_call" | custom-call | tf_op jit(solution)/shard_map/middle/pallas_call | solution.py:273
  159.3 15.8 %all-to-all-done.3.x_ref = f32[4,2,4,128,128]{4,3,2,1,0:T(8,128)S(1)} async-done(((f32[4,2,4,128,128]{4,3,2,1,0:T(8,128)}), f32[4,2,4,128,128]{4,3,2,1,0:T(8,128)S(1)}, u32[]{:S(2)}, u32[]{:S(2)}) %all-to-all-start.3) | async-done | bytes 2097184 | tf_op jit(solution)/shard_map/all_to_all | solution.py:293
  175.0 0.0 copy-start
  175.0 1.4 copy-done
  176.4 4.4 %all-to-all-start.7 = ((f32[4,2,4,128,128]{4,3,2,1,0:T(8,128)}), f32[4,2,4,128,128]{4,3,2,1,0:T(8,128)}, u32[]{:S(2)}, u32[]{:S(2)}) async-start(f32[4,2,4,128,128]{4,3,2,1,0:T(8,128)} %middle.3), calls=%async_computation.7 | async-start | bytes 4194304 | tf_op jit(solution)/shard_map/all_to_all | solution.py:293
  180.8 4.7 %gather_terms.2 = f32[8,2,128,128]{3,2,1,0:T(8,128)} custom-call(f32[2,4]{1,0:T(2,128)} %stack.7.power_ref, f32[4,2,4,128,128]{4,3,2,1,0:T(8,128)} %copy-done), custom_call_target="tpu_custom_call" | custom-call | tf_op jit(solution)/shard_map/gather_terms/pallas_call | solution.py:294
  185.5 19.8 %all-to-all-done.7.x_ref = f32[4,2,4,128,128]{4,3,2,1,0:T(8,128)} async-done(((f32[4,2,4,128,128]{4,3,2,1,0:T(8,128)}), f32[4,2,4,128,128]{4,3,2,1,0:T(8,128)}, u32[]{:S(2)}, u32[]{:S(2)}) %all-to-all-start.7) | async-done | bytes 2097184 | tf_op jit(solution)/shard_map/all_to_all | solution.py:293
  205.3 3.6 %all-to-all-start.4 = ((f32[8,2,128,128]{3,2,1,0:T(8,128)}), f32[8,2,128,128]{3,2,1,0:T(8,128)S(1)}, u32[]{:S(2)}, u32[]{:S(2)}) async-start(f32[8,2,128,128]{3,2,1,0:T(8,128)} %gather_terms.2), calls=%async_computation.4 | async-start | bytes 2097152 | tf_op jit(solution)/shard_map/all_to_all | solution.py:302
  208.8 4.7 %gather_terms.3 = f32[8,2,128,128]{3,2,1,0:T(8,128)} custom-call(f32[2,4]{1,0:T(2,128)} %stack.7.power_ref, f32[4,2,4,128,128]{4,3,2,1,0:T(8,128)} %all-to-all-done.7.x_ref), custom_call_target="tpu_custom_call" | custom-call | tf_op jit(solution)/shard_map/gather_terms/pallas_call | solution.py:294
  213.6 21.8 %all-to-all-done.4 = f32[8,2,128,128]{3,2,1,0:T(8,128)S(1)} async-done(((f32[8,2,128,128]{3,2,1,0:T(8,128)}), f32[8,2,128,128]{3,2,1,0:T(8,128)S(1)}, u32[]{:S(2)}, u32[]{:S(2)}) %all-to-all-start.4) | async-done | bytes 1048608 | tf_op jit(solution)/shard_map/all_to_all | solution.py:302
  235.3 0.0 copy-start.4
  235.3 30.8 %all_to_all.52 = f32[8,2,128,128]{3,2,1,0:T(8,128)} all-to-all(f32[8,2,128,128]{3,2,1,0:T(8,128)} %gather_terms.3), channel_id=1, replica_groups=mesh['chan'=4,'slab'=8] {'slab'}, dimensions={0} | all-to-all | bytes 2097152 | tf_op jit(solution)/shard_map/all_to_all | solution.py:302
  266.1 0.0 copy-done.4
  266.1 4.6 %rows_inverse.1 = f32[4,128,512]{2,1,0:T(8,128)} custom-call(bf16[2,256,256]{2,1,0:T(8,128)(2,1)} %constant.12.clone.back_ref.table_ref, f32[2,16,128]{2,1,0:T(8,128)} %constant.13.clone.twist_ref, f32[8,2,8,16,128]{4,3,2,1,0:T(8,128)} %bitcast.13, f32[8,2,8,16,128]{4,3,2,1,0:T(8,128)} %bitcast.14), custom_call_target="tpu_custom_call" | custom-call | tf_op jit(solution)/shard_map/rows_inverse/pallas_call | solution.py:305
  270.7 17.5 %all_to_all.53 = f32[4,128,512]{2,1,0:T(8,128)S(1)} all-to-all(f32[4,128,512]{2,1,0:T(8,128)} %rows_inverse.1), channel_id=1, replica_groups=mesh['chan'=4,'slab'=8] {'chan'}, dimensions={0} | all-to-all | bytes 2097152 | tf_op jit(solution)/shard_map/all_to_all | solution.py:312
  288.2 0.7 copy.10
  288.9 1.3 reshape.31
  (2 shorter events, 0.0 us)
Async XLA Ops:
  26.2 35.9 %copy-start.5 = (u32[32]{0:T(128)S(1)}, u32[32]{0:T(128)}, u32[]{:S(2)}) copy-start(u32[32]{0:T(128)} %constant.22) | copy-start | bytes 388
  57.9 30.1 %all-to-all-start.5 = ((f32[8,2,128,128]{3,2,1,0:T(8,128)}), f32[8,2,128,128]{3,2,1,0:T(8,128)S(1)}, u32[]{:S(2)}, u32[]{:S(2)}) async-start(f32[8,2,128,128]{3,2,1,0:T(8,128)} %bitcast.6), calls=%async_computation.5 | async-start | bytes 2097152 | tf_op jit(solution)/shard_map/all_to_all | solution.py:257
  87.9 3.6 %copy-start.3 = (f32[8,2,128,128]{3,2,1,0:T(8,128)}, f32[8,2,128,128]{3,2,1,0:T(8,128)S(1)}, u32[]{:S(2)}) copy-start(f32[8,2,128,128]{3,2,1,0:T(8,128)S(1)} %all-to-all-done.5.x_ref) | copy-start | bytes 3145732
  87.9 28.4 %all-to-all-start.2 = ((f32[4,2,4,128,128]{4,3,2,1,0:T(8,128)}), f32[4,2,4,128,128]{4,3,2,1,0:T(8,128)S(1)}, u32[]{:S(2)}, u32[]{:S(2)}) async-start(f32[4,2,4,128,128]{4,3,2,1,0:T(8,128)} %mix.2), calls=%async_computation.2 | async-start | bytes 4194304 | tf_op jit(solution)/shard_map/all_to_all | solution.py:268
  116.4 1.4 copy-start.2
  117.7 28.0 %all-to-all-start.6 = ((f32[4,2,4,128,128]{4,3,2,1,0:T(8,128)}), f32[4,2,4,128,128]{4,3,2,1,0:T(8,128)S(1)}, u32[]{:S(2)}, u32[]{:S(2)}) async-start(f32[4,2,4,128,128]{4,3,2,1,0:T(8,128)} %mix.3), calls=%async_computation.6 | async-start | bytes 4194304 | tf_op jit(solution)/shard_map/all_to_all | solution.py:268
  145.7 1.4 copy-start.1
  147.1 28.0 %all-to-all-start.3 = ((f32[4,2,4,128,128]{4,3,2,1,0:T(8,128)}), f32[4,2,4,128,128]{4,3,2,1,0:T(8,128)S(1)}, u32[]{:S(2)}, u32[]{:S(2)}) async-start(f32[4,2,4,128,128]{4,3,2,1,0:T(8,128)} %middle.2), calls=%async_computation.3 | async-start | bytes 4194304 | tf_op jit(solution)/shard_map/all_to_all | solution.py:293
  175.0 1.4 copy-start
  176.4 28.9 %all-to-all-start.7 = ((f32[4,2,4,128,128]{4,3,2,1,0:T(8,128)}), f32[4,2,4,128,128]{4,3,2,1,0:T(8,128)}, u32[]{:S(2)}, u32[]{:S(2)}) async-start(f32[4,2,4,128,128]{4,3,2,1,0:T(8,128)} %middle.3), calls=%async_computation.7 | async-start | bytes 4194304 | tf_op jit(solution)/shard_map/all_to_all | solution.py:293
  205.3 30.1 %all-to-all-start.4 = ((f32[8,2,128,128]{3,2,1,0:T(8,128)}), f32[8,2,128,128]{3,2,1,0:T(8,128)S(1)}, u32[]{:S(2)}, u32[]{:S(2)}) async-start(f32[8,2,128,128]{3,2,1,0:T(8,128)} %gather_terms.2), calls=%async_computation.4 | async-start | bytes 2097152 | tf_op jit(solution)/shard_map/all_to_all | solution.py:302
  235.3 30.8 %copy-start.4 = (f32[8,2,128,128]{3,2,1,0:T(8,128)}, f32[8,2,128,128]{3,2,1,0:T(8,128)S(1)}, u32[]{:S(2)}) copy-start(f32[8,2,128,128]{3,2,1,0:T(8,128)S(1)} %all-to-all-done.4) | copy-start | bytes 3145732
